TPU v7x, 512 devices: a whole 4x8x8 slice. The times are simulated.
512 devices in a mesh: section: 64 (over z, x, core), head: 8 (over y).
Axes of the slice: x: 4, y: 8, z: 8, core: 2. Of those that a mesh axis runs over, the one named last changes fastest.
Arguments:
- slice_rows: bfloat16 [8192, 4096], P('section', 'head'), may hold values from -6 to 6
- w_query: bfloat16 [4096, 4096], P(None, 'head'), may hold values from -0.09375 to 0.09375
- w_key: bfloat16 [4096, 1024], P(None, 'head'), may hold values from -0.09375 to 0.09375
- w_value: bfloat16 [4096, 1024], P(None, 'head'), may hold values from -0.09375 to 0.09375
- prefix_keys: bfloat16 [32768, 1024], P('section', 'head'), may hold values from -140 to 140
- prefix_values: bfloat16 [32768, 1024], P('section', 'head'), may hold values from -6 to 6
- prefix_blocks: int32 [64], replicated, may hold values from 1 to 2, as said below
Outputs:
- attention: bfloat16 [8192, 4096], P('section', 'head')
Inputs may be any that keep to these rules, and one draw needn't show every extreme that they name: `prefix_blocks`: every section holds at least one live block; in every draw some section holds 2 blocks.
All inputs are finite; a program needn't handle non-finite values.
Results may differ from a plain program's by a relative error of at most 0.012.
The roundings to bfloat16 on the way count: a program that leaves them out, or rounds other values in their place, can miss the bound.
Values may be sent and summed in bfloat16 or wider, within the bound.
A program may use at most 64 MiB of HBM per device.

v0:
```python
import functools
import math

import jax
import jax.numpy as jnp
from jax import lax
from jax.experimental import pallas as pl
from jax.experimental.pallas import tpu as pltpu
from jax.sharding import PartitionSpec as P

HEAD_DIM = 128
BLOCK = 256
REACH = 7
COLUMNS = 4
LAYERS = 8
RING = 8
MESH = pl.DeviceIdType.MESH

SPLIT = 8
ROWS = 2 * 512 // SPLIT
LOW, HIGH = tuple(range(SPLIT // 2)), tuple(range(SPLIT // 2, SPLIT))
LOW_FIRST, HIGH_FIRST = LOW + HIGH, HIGH + LOW
RELAY = 4
PIECES = 8
PIECE = 128 // PIECES


def clock(hop, piece):
    return 3.5 + 2.75 * hop + 2.75 / PIECES * piece


DEFERRED = clock(0, PIECES - 1)


def rows_of(piece):
    return pl.ds((piece // 2) * ROWS, ROWS)


def steps(first, each=5.6 / SPLIT):
    return [first + each * index for index in range(SPLIT)]


def arrivals(column):
    events = []

    def add(times, slot, order=LOW_FIRST, kinds=(0, 1), right=(), left=(), up=(), pair=True, prev=None):
        for time, piece in zip(times, order):
            events.append(
                dict(
                    time=time, slot=slot, kinds=kinds, piece=piece,
                    right=piece in right, left=piece in left, up=piece in up, pair=pair,
                    prev=slot >= column if prev is None else prev,
                )
            )

    every = LOW + HIGH
    direct, relayed = steps(3.5), steps(6.5)
    if column < 3:
        add(steps(7.0, 2.8 / SPLIT), column, kinds=(1,))
        order = HIGH_FIRST if column == 2 else LOW_FIRST
        add(direct, RELAY, order, up=every, pair=False, prev=False)
    if column == 0:
        add(relayed, 1)
        add(steps(7.1), 3, right=LOW)
        add(steps(8.3), 2)
    elif column == 1:
        add(direct, 0, right=LOW)
        add(relayed, 2, left=every)
        add(steps(9.5), 3, LOW)
        add(steps(8.3), 3, HIGH)
    elif column == 2:
        add(direct, 1, right=every)
        add(relayed, 3, HIGH_FIRST, left=HIGH)
        add(steps(8.0), 0, LOW)
        add(steps(8.0), 0, HIGH)
    else:
        add(steps(4.2), 3, right=every)
        add(direct, 2)
        add(direct, 0, HIGH_FIRST, left=HIGH)
        add(steps(8.0), 1)
    return sorted(events, key=lambda event: event["time"])


def gather_kernel(
    x_ref, wq_ref, wk_ref, wv_ref, pk_ref, pv_ref,
    q_ref, k_ref, v_ref, kv_ref,
    xbuf, xother, weights, acc, relay,
    w_sem, local_sem, x_send, x_recv, x_pair_send, x_pair_recv,
    right_send, left_send, up_send, own_send, relay_send, right_fwd, left_fwd, pair_send,
    slot_recv, relay_recv, pair_recv, ready,
):
    section = lax.axis_index("section")
    y = lax.axis_index("head")
    core = lax.rem(section, 2)
    x = lax.rem(lax.div(section, 2), COLUMNS)
    z = lax.div(section, 2 * COLUMNS)

    def at(layer, column, kind, ring=None):
        return ((layer * COLUMNS + column) * 2 + kind, y if ring is None else ring)

    x_right, x_left = lax.rem(x + 1, COLUMNS), lax.rem(x + COLUMNS - 1, COLUMNS)
    z_above, z_below = lax.rem(z + 1, LAYERS), lax.rem(z + LAYERS - 1, LAYERS)
    y_up, y_down = lax.rem(y + 1, RING), lax.rem(y + RING - 1, RING)
    right, left = at(z, x_right, 1), at(z, x_left, 1)
    above = at(z_above, x, 1)
    ways = (at(z, x, 1, y_up), at(z, x, 1, y_down))
    pair = at(z, x, 1 - core)

    def block_at(hop):
        return lax.rem(y + hop + RING, RING)

    visits = [0, -1, 1, -2, 2, -3, 3, 4]

    def start_weights(hop):
        start = pl.multiple_of(block_at(hop) * 512, 512)
        rows = pl.ds(start, 512)
        for source, first, size in ((wq_ref, 0, 512), (wk_ref, 512, 128), (wv_ref, 640, 128)):
            pltpu.make_async_copy(
                source.at[rows], weights.at[rows, first : first + size], w_sem.at[min(abs(hop), 1)]
            ).start()

    def wait_weights(index, blocks):
        rows = weights.at[: blocks * 512]
        pltpu.make_async_copy(rows, rows, w_sem.at[index]).wait()

    def project(hop):
        start = pl.multiple_of(block_at(hop) * 512, 512)
        part = jnp.dot(
            xbuf[block_at(hop)], weights[pl.ds(start, 512), :], preferred_element_type=jnp.float32
        )
        if hop == 0:
            acc[...] = part
        else:
            acc[...] += part

    def remote(source, target, send, recv, device):
        return pltpu.make_async_remote_copy(
            src_ref=source, dst_ref=target, send_sem=send, recv_sem=recv,
            device_id=device, device_id_type=MESH,
        )

    own_x = pltpu.make_async_copy(x_ref, xbuf.at[y], local_sem.at[0])
    own_x.start()
    start_weights(0)

    def tell(semaphore, device):
        pl.semaphore_signal(semaphore, inc=1, device_id=device, device_id_type=MESH)

    barrier = pltpu.get_barrier_semaphore()

    @pl.when(core == 1)
    def _():
        for kind in range(2):
            for device in (
                at(z, x, kind, y_up), at(z, x, kind, y_down),
                at(z, x_right, kind), at(z, x_left, kind),
            ):
                tell(barrier, device)

    tell(barrier, pair)

    @pl.when((z < LAYERS - 1) & ((core == 1) | (x == 3)))
    def _():
        tell(barrier, above)

    for hop in visits[1:]:
        start_weights(hop)
    pltpu.make_async_copy(pk_ref, kv_ref.at[8, 0], local_sem.at[1]).start()
    pltpu.make_async_copy(pv_ref, kv_ref.at[8, 1], local_sem.at[1]).start()
    below_count = jnp.where((core == 1) & (z > 0), jnp.where(x == 3, 2, 1), 0)
    pl.semaphore_wait(barrier, 5 + below_count)

    @pl.when((core == 1) & (z > 0))
    def _():
        tell(ready, at(z_below, x, 1))

        @pl.when(x == 3)
        def _():
            tell(ready, at(z_below, x, 0))

    def received(here, semaphore):
        remote(here, here, own_send, semaphore, pair).wait_recv()

    def sent(here, semaphore):
        remote(here, here, semaphore, pair_recv, pair).wait_send()

    def pieces_of(count):
        return kv_ref.at[0, 0, : ROWS * count] if count < 3 else kv_ref.at[: count // SPLIT]

    def rows_at(piece):
        return pl.ds(piece * PIECE, PIECE)

    def x_own(way, piece, kind):
        target = xother if kind == 0 else xbuf
        return remote(
            x_ref.at[rows_at(piece)], target.at[y, rows_at(piece)],
            x_send.at[way], x_recv.at[way, piece], ways[way],
        )

    def x_origin(way, hop):
        return block_at(-hop - 1 if way == 0 else hop + 1)

    def x_piece(way, hop, piece, kind):
        return (xother if kind == 0 else xbuf).at[x_origin(way, hop), rows_at(piece)]

    def x_forward(way, hop, piece, kind):
        here = x_piece(way, hop, piece, kind)
        index = (hop + 1) * PIECES + piece
        return remote(here, here, x_send.at[way], x_recv.at[way, index], ways[way])

    def x_hand(way, hop, piece):
        rows = rows_at(piece)
        return remote(
            xother.at[x_origin(way, hop), rows], xbuf.at[x_origin(way, hop), rows],
            x_pair_send, x_pair_recv.at[min(hop * 2 + way, 6)], pair,
        )

    def travels(way, hop, piece):
        return hop < 3 or (hop == 3 and piece // (PIECES // 2) == way)

    def own_piece(piece):
        return (pk_ref if piece % 2 == 0 else pv_ref).at[rows_of(piece)]

    def slot_piece(column, kind, piece):
        return kv_ref.at[column * 2 + kind, piece % 2, rows_of(piece)]

    def relay_piece(kind, piece):
        return relay.at[kind, piece % 2, rows_of(piece)]

    def send_right(kind, piece, column):
        return remote(
            own_piece(piece), slot_piece(column, kind, piece),
            right_send, slot_recv.at[column, piece], right,
        )

    def send_left(kind, piece, column):
        if column == 0:
            target, arrived = slot_piece(0, kind, piece), slot_recv.at[0, piece]
        else:
            target, arrived = relay_piece(kind, piece), relay_recv.at[piece]
        return remote(own_piece(piece), target, left_send, arrived, left)

    def send_up(kind, piece):
        if kind == 0:
            target, arrived = relay_piece(2, piece), slot_recv.at[x, piece]
        else:
            target, arrived = slot_piece(x, 1, piece), slot_recv.at[x, piece]
        return remote(own_piece(piece), target, up_send, arrived, above)

    def send_pair(piece):
        return remote(
            own_piece(piece), slot_piece(x, 0, piece),
            own_send, pair_recv, pair,
        )

    def first_sends(kind, column):
        leftward = HIGH_FIRST if column in (0, 3) else LOW_FIRST
        for index in range(SPLIT):
            yield column > 0, functools.partial(send_left, kind, leftward[index], column)
            if column < 3:
                yield False, functools.partial(send_right, kind, index, column)

    def source_of(event, column, kind):
        if event["slot"] == RELAY:
            return relay_piece(kind, event["piece"])
        if column == 3 and event["slot"] == 3 and kind == 0:
            return relay_piece(2, event["piece"])
        return slot_piece(event["slot"], kind, event["piece"])

    def sends_of(event, column, upward):
        for kind in event["kinds"]:
            piece, slot = event["piece"], event["slot"]
            source = source_of(event, column, kind)
            if upward:
                if event["up"]:
                    yield remote(
                        source, slot_piece(column + 1, kind, piece), relay_send,
                        slot_recv.at[column + 1, piece], above,
                    )
                continue
            if slot == RELAY:
                continue
            target, arrived = slot_piece(slot, kind, piece), slot_recv.at[slot, piece]
            if event["right"]:
                yield remote(source, target, right_fwd, arrived, right)
            if event["left"]:
                yield remote(source, target, left_fwd, arrived, left)
            if event["pair"] and (slot != column or kind == 1):
                yield remote(source, target, pair_send, pair_recv, pair)

    def count(column, what, prevs):
        total = 0
        for event in arrivals(column):
            if event[what] and (prevs or not event["prev"]):
                kinds = (1,) if what == "pair" and event["slot"] == column else event["kinds"]
                total += len(kinds)
        return total

    def guarded(condition, run):
        if condition is None:
            run()
        else:
            pl.when(condition)(run)

    def start_first(kind):
        for piece in range(PIECES):
            for way in range(2):
                x_own(way, piece, kind).start()
        for column in range(COLUMNS):

            @pl.when(x == column)
            def _():
                plain = [make for needs, make in first_sends(kind, column) if not needs]
                needing = [make for needs, make in first_sends(kind, column) if needs]
                if needing:

                    @pl.when(z < LAYERS - 1)
                    def _():
                        for make in needing:
                            make().start()

                for make in plain:
                    make().start()

    def finish_first(kind):
        @pl.when((x == 0) | (z < LAYERS - 1))
        def _():
            sent(pieces_of(SPLIT), left_send)

        @pl.when(x < 3)
        def _():
            sent(pieces_of(SPLIT), right_send)

        @pl.when((z < LAYERS - 1) & (x == 3) if kind == 0 else z < LAYERS - 1)
        def _():
            sent(pieces_of(SPLIT), up_send)

    @pl.when(z == 0)
    def _():
        for column in range(COLUMNS):

            @pl.when(x == column)
            def _():
                for slot in range(column * 2 + 2, COLUMNS * 2):
                    kv_ref[slot] = jnp.zeros((2, 512, HEAD_DIM), jnp.bfloat16)

                @pl.when(core == 0)
                def _():
                    kv_ref[column * 2 + 1] = jnp.zeros((2, 512, HEAD_DIM), jnp.bfloat16)

    @pl.when(core == 0)
    def _():
        start_first(0)
        for piece in range(SPLIT):
            send_pair(piece).start()
        own_x.wait()
        wait_weights(0, 1)
        project(0)

        @pl.when((x == 3) & (z < LAYERS - 1))
        def _():
            pl.semaphore_wait(ready, 1)
            for piece in range(SPLIT):
                send_up(0, piece).start()

        wait_weights(1, 7)
        for index, hop in enumerate(visits[1:]):
            received(xbuf.at[0], x_pair_recv.at[index])
            project(hop)

        @pl.when(z > 0)
        def _():
            received(pieces_of(7 * SPLIT), pair_recv)

        for column in range(1, COLUMNS):

            @pl.when((z == 0) & (x == column))
            def _():
                received(pieces_of(2 * SPLIT * column), pair_recv)

        finish_first(0)
        sent(pieces_of(SPLIT), own_send)
        for way in range(2):
            sent(xbuf.at[0], x_send.at[way])

    schedules = [arrivals(column) for column in range(COLUMNS)]

    def handle(event, column):
        def run():
            semaphore = (relay_recv if event["slot"] == RELAY else slot_recv.at[event["slot"]]).at[event["piece"]]
            received(pieces_of(len(event["kinds"])), semaphore)
            if event["up"]:
                held = event["time"] <= DEFERRED

                @pl.when((z > 0) & (z < LAYERS - 1) if held else z < LAYERS - 1)
                def _():
                    for copy in sends_of(event, column, True):
                        copy.start()

            for copy in sends_of(event, column, False):
                copy.start()

        whole = event["slot"] == RELAY and event["up"]
        guarded(z < LAYERS - 1 if whole else z > 0 if event["prev"] else None, run)

    def prefixes(until):
        for column in range(COLUMNS):
            due = [event for event in schedules[column] if event["time"] <= until]
            if not due:
                continue
            schedules[column] = schedules[column][len(due) :]

            @pl.when(x == column)
            def _():
                for event in due:
                    handle(event, column)

    def lowest_goes_up():
        @pl.when(z == 0)
        def _():
            pl.semaphore_wait(ready, 1)
            for piece in range(SPLIT):
                send_up(1, piece).start()

    def lowest_relays():
        for column in range(0, COLUMNS - 1):

            @pl.when((z == 0) & (x == column))
            def _():
                for event in arrivals(column):
                    if event["up"] and event["time"] <= DEFERRED:
                        for copy in sends_of(event, column, True):
                            copy.start()

    @pl.when(core == 1)
    def _():
        start_first(1)

        @pl.when((z > 0) & (z < LAYERS - 1))
        def _():
            pl.semaphore_wait(ready, 1)
            for piece in range(SPLIT):
                send_up(1, piece).start()

        own_x.wait()
        wait_weights(0, 1)
        project(0)
        lowest_goes_up()
        for hop in range(4):
            for piece in range(PIECES):
                if hop == 3 and piece >= PIECES // 2:
                    continue
                for way in range(2):
                    this = piece if hop < 3 or way == 0 else piece + PIECES // 2
                    received(xbuf.at[0, : 2 * PIECE], x_recv.at[way, hop * PIECES + this])
                    for kind in range(2):
                        if travels(way, hop + 1, this):
                            x_forward(way, hop, this, kind).start()
                    x_hand(way, hop, this).start()
                prefixes(clock(hop, piece))
                if hop == 0 and piece == PIECES - 1:
                    lowest_relays()
                    wait_weights(1, 7)
                if hop > 0 and piece == 0:
                    project(-hop)
                if hop > 0 and piece == 1:
                    project(hop)
        project(4)
        prefixes(99.0)
        received(pieces_of(SPLIT), pair_recv)

        finish_first(1)
        for way in range(2):
            sent(xbuf.at[:6], x_send.at[way])
        sent(xbuf.at[:7], x_pair_send)
        for column in range(COLUMNS):

            @pl.when(x == column)
            def _():
                for condition, prevs in ((z > 0, True), (z == 0, False)):

                    @pl.when(condition)
                    def _():
                        for what, semaphore in (("pair", pair_send), ("right", right_fwd), ("left", left_fwd)):
                            total = count(column, what, prevs)
                            if total:
                                sent(pieces_of(total), semaphore)

                if column < 3:

                    @pl.when(z < LAYERS - 1)
                    def _():
                        sent(pieces_of(2 * SPLIT), relay_send)

    for group in range(4):
        q_ref[group * 128 : (group + 1) * 128, :] = acc[:, group * 128 : (group + 1) * 128].astype(jnp.bfloat16)
    k_ref[...] = acc[:, 512:640].astype(jnp.bfloat16)
    v_ref[...] = acc[:, 640:768].astype(jnp.bfloat16)
    pltpu.make_async_copy(kv_ref.at[8], kv_ref.at[8], local_sem.at[1]).wait()


def gather(slice_rows, w_query, w_key, w_value, prefix_keys, prefix_values):
    bf16, f32 = jnp.bfloat16, jnp.float32
    dma = pltpu.SemaphoreType.DMA
    anywhere = pl.BlockSpec(memory_space=pltpu.HBM)
    vmem = pl.BlockSpec(memory_space=pltpu.VMEM)
    return pl.pallas_call(
        gather_kernel,
        out_shape=(
            pltpu.VMEM((512, HEAD_DIM), bf16),
            pltpu.VMEM((128, HEAD_DIM), bf16),
            pltpu.VMEM((128, HEAD_DIM), bf16),
            pltpu.VMEM((9, 2, 512, HEAD_DIM), bf16),
        ),
        in_specs=[anywhere] * 6,
        out_specs=(vmem,) * 4,
        scratch_shapes=[
            pltpu.VMEM((RING, 128, 512), bf16),
            pltpu.VMEM((RING, 128, 512), bf16),
            pltpu.VMEM((4096, 768), bf16),
            pltpu.VMEM((128, 768), f32),
            pltpu.VMEM((3, 2, 512, HEAD_DIM), bf16),
            dma((2,)), dma((2,)),
            dma((2,)), dma((2, 4 * PIECES)), dma, dma((7,)),
            dma, dma, dma, dma, dma, dma, dma, dma,
            dma((4, SPLIT)), dma((SPLIT,)), dma, pltpu.SemaphoreType.REGULAR,
        ],
        compiler_params=pltpu.CompilerParams(
            collective_id=0, has_side_effects=True, vmem_limit_bytes=58 * 1024 * 1024
        ),
        name="gather",
    )(slice_rows, w_query, w_key, w_value, prefix_keys, prefix_values)


def scores_of(keys, queries):
    return lax.dot_general(
        keys, queries, (((1,), (1,)), ((), ())), preferred_element_type=jnp.float32
    )


def weigh(values, weights):
    return lax.dot_general(
        values, weights, (((0,), (0,)), ((), ())), preferred_element_type=jnp.float32
    )


def attend_kernel(
    blocks_ref, q_ref, k_ref, v_ref, kv_ref, out_ref, scores, m_ref, l_ref, o_ref, pb_ref, out, pb_sem, out_sem
):
    section = lax.axis_index("section")
    factor = math.log2(math.e) / math.sqrt(HEAD_DIM)
    never = 1e30
    live = pltpu.make_async_copy(blocks_ref, pb_ref, pb_sem)
    live.start()
    queries = q_ref[...]

    def slot_of(offset):
        return 8 if offset == 0 else lax.rem(section - offset + 64, 8)

    key_row = lax.broadcasted_iota(jnp.int32, (128, 512), 0)
    query_row = lax.broadcasted_iota(jnp.int32, (128, 512), 1) % 128
    own = jnp.where(key_row <= query_row, scores_of(k_ref[...], queries), -never)
    top = jnp.max(own, axis=0, keepdims=True)
    for offset in range(REACH + 1):
        part = scores_of(kv_ref[slot_of(offset), 0, :BLOCK, :], queries)
        scores[offset] = part
        peak = jnp.max(part, axis=0, keepdims=True)
        top = jnp.maximum(top, jnp.where(section >= offset, peak, -never))
    weights = jnp.exp2((own - top) * factor)
    total = jnp.sum(weights, axis=0, keepdims=True)
    result = weigh(v_ref[...], weights.astype(jnp.bfloat16))
    for offset in range(REACH + 1):
        shift = jnp.where(section >= offset, top, never)
        weights = jnp.exp2((scores[offset] - shift) * factor)
        total += jnp.sum(weights, axis=0, keepdims=True)
        result += weigh(kv_ref[slot_of(offset), 1, :BLOCK, :], weights.astype(jnp.bfloat16))
    m_ref[...] = top
    l_ref[...] = total
    o_ref[...] = result
    live.wait()

    for offset in range(REACH + 1):
        blocks = pb_ref[jnp.maximum(section - offset, 0)]

        @pl.when((section >= offset) & (blocks > 1))
        def _():
            part = scores_of(kv_ref[slot_of(offset), 0, BLOCK:, :], queries)
            before = m_ref[...]
            after = jnp.maximum(before, jnp.max(part, axis=0, keepdims=True))
            keep = jnp.exp2((before - after) * factor)
            weights = jnp.exp2((part - after) * factor)
            m_ref[...] = after
            l_ref[...] = l_ref[...] * keep + jnp.sum(weights, axis=0, keepdims=True)
            o_ref[...] = o_ref[...] * keep + weigh(
                kv_ref[slot_of(offset), 1, BLOCK:, :], weights.astype(jnp.bfloat16)
            )

    final = o_ref[...] / l_ref[...]
    for group in range(4):
        columns = slice(group * 128, (group + 1) * 128)
        out[:, columns] = final[:, columns].T.astype(jnp.bfloat16)
    copy = pltpu.make_async_copy(out, out_ref, out_sem)
    copy.start()
    copy.wait()


def attend(prefix_blocks, queries, own_keys, own_values, kv):
    vmem = pl.BlockSpec(memory_space=pltpu.VMEM)
    return pl.pallas_call(
        attend_kernel,
        out_shape=jax.ShapeDtypeStruct((128, 512), jnp.bfloat16),
        in_specs=[pl.BlockSpec(memory_space=pltpu.HBM)] + [vmem] * 4,
        out_specs=pl.BlockSpec(memory_space=pltpu.HBM),
        scratch_shapes=[
            pltpu.VMEM((REACH + 1, BLOCK, 512), jnp.float32),
            pltpu.VMEM((1, 512), jnp.float32),
            pltpu.VMEM((1, 512), jnp.float32),
            pltpu.VMEM((HEAD_DIM, 512), jnp.float32),
            pltpu.SMEM((64,), jnp.int32),
            pltpu.VMEM((128, 512), jnp.bfloat16),
            pltpu.SemaphoreType.DMA,
            pltpu.SemaphoreType.DMA,
        ],
        compiler_params=pltpu.CompilerParams(vmem_limit_bytes=24 * 1024 * 1024),
        name="attend",
    )(prefix_blocks, queries, own_keys, own_values, kv)


def on_device(slice_rows, w_query, w_key, w_value, prefix_keys, prefix_values, prefix_blocks):
    queries, own_keys, own_values, kv = gather(
        slice_rows, w_query, w_key, w_value, prefix_keys, prefix_values
    )
    return attend(prefix_blocks, queries, own_keys, own_values, kv)


def solution(mesh):
    in_specs = (
        P("section", "head"),
        P(None, "head"),
        P(None, "head"),
        P(None, "head"),
        P("section", "head"),
        P("section", "head"),
        P(),
    )
    out_specs = P("section", "head")
    return jax.shard_map(
        on_device, mesh=mesh, in_specs=in_specs, out_specs=out_specs, check_vma=False
    )
```

profile of v0, /device:TPU:65, one launch (start us, length us, event | category | flops | bytes accessed | tf_op | source)
XLA Modules:
  0.0 25.5 jit_solution(13024490781952509950)
XLA Ops:
  0.0 0.0 copy-start
  0.0 22.6 %gather.1 = (bf16[512,128]{1,0:T(8,128)(2,1)S(1)}, bf16[128,128]{1,0:T(8,128)(2,1)S(1)}, bf16[128,128]{1,0:T(8,128)(2,1)S(1)}, bf16[9,2,512,128]{3,2,1,0:T(8,128)(2,1)S(1)}) custom-call(bf16[128,512]{1,0:T(8,128)(2,1)} %x_ref.1, bf16[4096,512]{1,0:T(8,128)(2,1)} %wq_ref.1, bf16[4096,128]{1,0:T(8,128)(2,1)} %wk_ref.1, bf16[4096,128]{1,0:T(8,128)(2,1)} %wv_ref.1, ...), custom_call_target="tpu_custom_call" | custom-call | tf_op jit(solution)/shard_map/gather/pallas_call | solution.py:507
  22.6 0.0 copy-done
  22.7 2.9 %attend.1 = bf16[128,512]{1,0:T(8,128)(2,1)} custom-call(s32[64]{0:T(128)S(1)} %copy-done, bf16[512,128]{1,0:T(8,128)(2,1)S(1)} %get-tuple-element.9.q_ref, bf16[128,128]{1,0:T(8,128)(2,1)S(1)} %get-tuple-element.10.k_ref, bf16[128,128]{1,0:T(8,128)(2,1)S(1)} %get-tuple-element.11.v_ref, bf16[9,2,512,128]{3,2,1,0:T(8,128)(2,1)S(1)} %get-tuple-element.12.kv_ref), custom_call_target="tpu_custom_call" | custom-call | tf_op jit(solution)/shard_map/attend/pallas_call | solution.py:609
Async XLA Ops:
  0.0 22.7 %copy-start = (s32[64]{0:T(128)S(1)}, s32[64]{0:T(128)}, u32[]{:S(2)}) copy-start(s32[64]{0:T(128)} %blocks_ref.1) | copy-start | bytes 772
where the time goes:
time: 25.7 us; the launch traced here: 25.5 us
  Pallas kernels  25.5 us (99%)
    pallas_call x1, Pallas kernels, gather(): pl.pallas_call(gather_kernel, out_shape=(pltpu.VMEM((512, HEAD_DIM), bf16...  22.6 us
    pallas_call x1, Pallas kernels, attend(): pl.pallas_call(attend_kernel, out_shape=jax.ShapeDtypeStruct((128, 512),...  2.85 us

commit v1 on v0

--- a/solution.py
+++ b/solution.py
@@ -133,6 +133,12 @@
         else:
             acc[...] += part
 
+    def write_projected():
+        for group in range(4):
+            q_ref[group * 128 : (group + 1) * 128, :] = acc[:, group * 128 : (group + 1) * 128].astype(jnp.bfloat16)
+        k_ref[...] = acc[:, 512:640].astype(jnp.bfloat16)
+        v_ref[...] = acc[:, 640:768].astype(jnp.bfloat16)
+
     def remote(source, target, send, recv, device):
         return pltpu.make_async_remote_copy(
             src_ref=source, dst_ref=target, send_sem=send, recv_sem=recv,
@@ -367,6 +373,7 @@
         for index, hop in enumerate(visits[1:]):
             received(xbuf.at[0], x_pair_recv.at[index])
             project(hop)
+        write_projected()
 
         @pl.when(z > 0)
         def _():
@@ -467,6 +474,7 @@
                     project(hop)
         project(4)
         prefixes(99.0)
+        write_projected()
         received(pieces_of(SPLIT), pair_recv)
 
         finish_first(1)
@@ -492,10 +500,6 @@
                     def _():
                         sent(pieces_of(2 * SPLIT), relay_send)
 
-    for group in range(4):
-        q_ref[group * 128 : (group + 1) * 128, :] = acc[:, group * 128 : (group + 1) * 128].astype(jnp.bfloat16)
-    k_ref[...] = acc[:, 512:640].astype(jnp.bfloat16)
-    v_ref[...] = acc[:, 640:768].astype(jnp.bfloat16)
     pltpu.make_async_copy(kv_ref.at[8], kv_ref.at[8], local_sem.at[1]).wait()
 
 

time: 25.7 us -> 26.2 us (1.019)
  the two profiles are of different devices: /device:TPU:65 before, /device:TPU:257 now
where the time goes in v1:
time: 26.2 us; the launch traced here: 26.1 us
  Pallas kernels  26.1 us (100%)
    pallas_call x1, Pallas kernels, gather(): pl.pallas_call(gather_kernel, out_shape=(pltpu.VMEM((512, HEAD_DIM), bf16...  22.3 us
    pallas_call x1, Pallas kernels, attend(): pl.pallas_call(attend_kernel, out_shape=jax.ShapeDtypeStruct((128, 512),...  3.84 us

profile of v1, /device:TPU:257, one launch (start us, length us, event | category | flops | bytes accessed | tf_op | source)
XLA Modules:
  0.0 26.1 jit_solution(3740607227751143575)
XLA Ops:
  0.0 0.0 copy-start
  0.0 22.3 %gather.1 = (bf16[512,128]{1,0:T(8,128)(2,1)S(1)}, bf16[128,128]{1,0:T(8,128)(2,1)S(1)}, bf16[128,128]{1,0:T(8,128)(2,1)S(1)}, bf16[9,2,512,128]{3,2,1,0:T(8,128)(2,1)S(1)}) custom-call(bf16[128,512]{1,0:T(8,128)(2,1)} %x_ref.1, bf16[4096,512]{1,0:T(8,128)(2,1)} %wq_ref.1, bf16[4096,128]{1,0:T(8,128)(2,1)} %wk_ref.1, bf16[4096,128]{1,0:T(8,128)(2,1)} %wv_ref.1, ...), custom_call_target="tpu_custom_call" | custom-call | tf_op jit(solution)/shard_map/gather/pallas_call | solution.py:511
  22.3 0.0 copy-done
  22.3 3.8 %attend.1 = bf16[128,512]{1,0:T(8,128)(2,1)} custom-call(s32[64]{0:T(128)S(1)} %copy-done, bf16[512,128]{1,0:T(8,128)(2,1)S(1)} %get-tuple-element.9.q_ref, bf16[128,128]{1,0:T(8,128)(2,1)S(1)} %get-tuple-element.10.k_ref, bf16[128,128]{1,0:T(8,128)(2,1)S(1)} %get-tuple-element.11.v_ref, bf16[9,2,512,128]{3,2,1,0:T(8,128)(2,1)S(1)} %get-tuple-element.12.kv_ref), custom_call_target="tpu_custom_call" | custom-call | tf_op jit(solution)/shard_map/attend/pallas_call | solution.py:613
Async XLA Ops:
  0.0 22.3 %copy-start = (s32[64]{0:T(128)S(1)}, s32[64]{0:T(128)}, u32[]{:S(2)}) copy-start(s32[64]{0:T(128)} %blocks_ref.1) | copy-start | bytes 772

commit v2 on v1

--- a/solution.py
+++ b/solution.py
@@ -146,8 +146,6 @@
         )
 
     own_x = pltpu.make_async_copy(x_ref, xbuf.at[y], local_sem.at[0])
-    own_x.start()
-    start_weights(0)
 
     def tell(semaphore, device):
         pl.semaphore_signal(semaphore, inc=1, device_id=device, device_id_type=MESH)
@@ -169,7 +167,8 @@
     def _():
         tell(barrier, above)
 
-    for hop in visits[1:]:
+    own_x.start()
+    for hop in visits:
         start_weights(hop)
     pltpu.make_async_copy(pk_ref, kv_ref.at[8, 0], local_sem.at[1]).start()
     pltpu.make_async_copy(pv_ref, kv_ref.at[8, 1], local_sem.at[1]).start()
@@ -195,6 +194,9 @@
 
     def rows_at(piece):
         return pl.ds(piece * PIECE, PIECE)
+
+    def x_index(hop, piece):
+        return hop * PIECES + (piece % (PIECES // 2) if hop == 3 else piece)
 
     def x_own(way, piece, kind):
         target = xother if kind == 0 else xbuf
@@ -211,7 +213,7 @@
 
     def x_forward(way, hop, piece, kind):
         here = x_piece(way, hop, piece, kind)
-        index = (hop + 1) * PIECES + piece
+        index = x_index(hop + 1, piece)
         return remote(here, here, x_send.at[way], x_recv.at[way, index], ways[way])
 
     def x_hand(way, hop, piece):
@@ -459,7 +461,7 @@
                     continue
                 for way in range(2):
                     this = piece if hop < 3 or way == 0 else piece + PIECES // 2
-                    received(xbuf.at[0, : 2 * PIECE], x_recv.at[way, hop * PIECES + this])
+                    received(xbuf.at[0, : 2 * PIECE], x_recv.at[way, x_index(hop, this)])
                     for kind in range(2):
                         if travels(way, hop + 1, this):
                             x_forward(way, hop, this, kind).start()
@@ -525,7 +527,7 @@
             pltpu.VMEM((128, 768), f32),
             pltpu.VMEM((3, 2, 512, HEAD_DIM), bf16),
             dma((2,)), dma((2,)),
-            dma((2,)), dma((2, 4 * PIECES)), dma, dma((7,)),
+            dma((2,)), dma((2, 3 * PIECES + PIECES // 2)), dma, dma((7,)),
             dma, dma, dma, dma, dma, dma, dma, dma,
             dma((4, SPLIT)), dma((SPLIT,)), dma, pltpu.SemaphoreType.REGULAR,
         ],

time: 26.2 us -> 25.5 us (0.973)
  the two profiles are of different devices: /device:TPU:257 before, /device:TPU:65 now
where the time goes in v2:
time: 25.5 us; the launch traced here: 25.4 us
  Pallas kernels  25.4 us (100%)
    pallas_call x1, Pallas kernels, gather(): pl.pallas_call(gather_kernel, out_shape=(pltpu.VMEM((512, HEAD_DIM), bf16...  22.5 us
    pallas_call x1, Pallas kernels, attend(): pl.pallas_call(attend_kernel, out_shape=jax.ShapeDtypeStruct((128, 512),...  2.86 us

profile of v2, /device:TPU:65, one launch (start us, length us, event | category | flops | bytes accessed | tf_op | source)
XLA Modules:
  0.0 25.4 jit_solution(4009383352211939777)
XLA Ops:
  0.0 0.0 copy-start
  0.0 22.5 %gather.1 = (bf16[512,128]{1,0:T(8,128)(2,1)S(1)}, bf16[128,128]{1,0:T(8,128)(2,1)S(1)}, bf16[128,128]{1,0:T(8,128)(2,1)S(1)}, bf16[9,2,512,128]{3,2,1,0:T(8,128)(2,1)S(1)}) custom-call(bf16[128,512]{1,0:T(8,128)(2,1)} %x_ref.1, bf16[4096,512]{1,0:T(8,128)(2,1)} %wq_ref.1, bf16[4096,128]{1,0:T(8,128)(2,1)} %wk_ref.1, bf16[4096,128]{1,0:T(8,128)(2,1)} %wv_ref.1, ...), custom_call_target="tpu_custom_call" | custom-call | tf_op jit(solution)/shard_map/gather/pallas_call | solution.py:513
  22.5 0.0 copy-done
  22.6 2.9 %attend.1 = bf16[128,512]{1,0:T(8,128)(2,1)} custom-call(s32[64]{0:T(128)S(1)} %copy-done, bf16[512,128]{1,0:T(8,128)(2,1)S(1)} %get-tuple-element.9.q_ref, bf16[128,128]{1,0:T(8,128)(2,1)S(1)} %get-tuple-element.10.k_ref, bf16[128,128]{1,0:T(8,128)(2,1)S(1)} %get-tuple-element.11.v_ref, bf16[9,2,512,128]{3,2,1,0:T(8,128)(2,1)S(1)} %get-tuple-element.12.kv_ref), custom_call_target="tpu_custom_call" | custom-call | tf_op jit(solution)/shard_map/attend/pallas_call | solution.py:615
Async XLA Ops:
  0.0 22.5 %copy-start = (s32[64]{0:T(128)S(1)}, s32[64]{0:T(128)}, u32[]{:S(2)}) copy-start(s32[64]{0:T(128)} %blocks_ref.1) | copy-start | bytes 772
